TPU v7x, 16 devices: a whole 2x2x2 slice. The times are simulated.
16 devices in a mesh: rep: 1, dp: 16 (over x, y, z, core).
Axes of the slice: x: 2, y: 2, z: 2, core: 2. Of those that a mesh axis runs over, the one named last changes fastest.
Arguments:
- x: bfloat16 [16, 2048, 1024], P(('rep', 'dp'))
- dy: bfloat16 [16, 2048, 1024], P(('rep', 'dp'))
- w_gate: bfloat16 [2, 1024, 6144], P(None, 'dp')
- w_up: bfloat16 [2, 1024, 6144], P(None, 'dp')
- w_down: bfloat16 [2, 6144, 1024], P(None, 'dp')
Outputs:
- output 1: bfloat16 [16, 2048, 1024], P(('rep', 'dp'))
- output 2: bfloat16 [2, 1024, 6144], P('rep', 'dp')
- output 3: bfloat16 [2, 1024, 6144], P('rep', 'dp')
- output 4: bfloat16 [2, 6144, 1024], P('rep', 'dp')
All inputs are finite; a program needn't handle non-finite values.
Results may differ from a plain program's by a relative error of at most 0.018.
Values are sent between devices in bfloat16 or wider.
A program may use at most 2 GiB of HBM per device.

v0:
```python
import jax
import jax.numpy as jnp
from jax import lax

NAMES = ("w_gate", "w_up", "w_down")


def matmul(a, w):
    return jnp.dot(a, w, preferred_element_type=jnp.float32).astype(jnp.bfloat16)


def normed(h):
    wide = h.astype(jnp.float32)
    scale = lax.rsqrt(jnp.mean(wide**2, -1, keepdims=True) + 1e-6)
    return (wide * scale).astype(jnp.bfloat16)


def layer(h, w):
    a = normed(h)
    gate = jnp.dot(a, w["w_gate"], preferred_element_type=jnp.float32)
    up = jnp.dot(a, w["w_up"], preferred_element_type=jnp.float32)
    return h + matmul((jax.nn.silu(gate) * up).astype(jnp.bfloat16), w["w_down"])


def stack(weights, h):
    for number in range(weights["w_gate"].shape[0]):
        h = layer(h, {name: w[number] for name, w in weights.items()})
    return h


def solution(mesh):
    groups = mesh.shape["rep"]

    def step(x, dy, *weights):
        shape = x.shape
        x, dy = (t.reshape(groups, -1, *t.shape[1:]) for t in (x, dy))

        def of_a_group(x, dy):
            _, back = jax.vjp(stack, dict(zip(NAMES, weights, strict=True)), x)
            by_weights, by_x = back(dy)
            return (by_x, *(by_weights[name] for name in NAMES))

        by_x, *by_weights = jax.vmap(of_a_group)(x, dy)
        return (by_x.reshape(shape), *(t.reshape(-1, *t.shape[2:]) for t in by_weights))

    return step
```

profile of v0, /device:TPU:0, one launch (start us, length us, event | category | flops | bytes accessed | tf_op | source)
XLA Modules:
  0.0 2987.5 jit_solution(4922775934838699815)
XLA Ops:
  45.1 260.6 %while.13 = (bf16[1,2048,1024]{2,1,0:T(8,128)(2,1)}, bf16[1,384,1024]{2,1,0:T(8,128)(2,1)}, bf16[1,2048,6144]{1,2,0:T(8,128)(2,1)}, bf16[1,384,1024]{2,1,0:T(8,1...) while((bf16[1,2048,1024]{2,1,0:T(8,128)(2,1)}, ...), condition=%wide.windowed_dot_general_cond_ag, body=%wide.windowed_dot_general_body_ag.sunk | while | flops 6444023808 | bytes 42992156 | solution.py:9
  78.9 17.5 collective-permute-start.3
  99.0 21.8 collective-permute-start.2
  163.6 24.9 collective-permute-start.2
  280.2 25.6 collective-permute-done.3
  305.8 32.8 %copy.2 = bf16[1,2048,6144]{2,1,0:T(8,128)(2,1)} copy(bf16[1,2048,6144]{1,2,0:T(8,128)(2,1)} %get-tuple-element.42) | data formatting | bytes 50331648 | tf_op jit(solution)/vmap(transpose(jvp()))/dot_general | solution.py:9
  338.5 35.4 %fusion.198 = f32[2048,6144]{1,0:T(8,128)} fusion(bf16[1,1024,6144]{2,1,0:T(8,128)(2,1)} %all-gather.27.cloned.1.call-done, bf16[1,2048,1024]{1,2,0:T(8,128)(2,1)} %fusion.205), kind=kOutput, calls=%fused_computation.245 | convolution fusion | flops 25769803776 | bytes 67108864 | tf_op jit(solution)/vmap(jvp())/dot_general | solution.py:20
  374.0 56.0 %fusion.180 = (bf16[1,2048,6144]{2,1,0:T(8,128)(2,1)}, f32[2048,6144]{1,0:T(8,128)}) fusion(f32[2048,6144]{1,0:T(8,128)} %fusion.198, bf16[1,1024,6144]{2,1,0:T(8,128)(2,1)} %all-gather.29.cloned.1.call-done, bf16[1,2048,1024]{1,2,0:T(8,128)(2,1)} %fusion.205), kind=kOutput, calls=%fused_computation.215 | convolution fusion | flops 25845301248 | bytes 142606336 | tf_op jit(solution)/vmap(jvp())/dot_general | solution.py:21
  429.9 32.7 %copy.6 = bf16[1,2048,6144]{1,2,0:T(8,128)(2,1)} copy(bf16[1,2048,6144]{2,1,0:T(8,128)(2,1)} %get-tuple-element.281) | data formatting | bytes 50331648
  462.7 46.6 %fusion.207 = (f32[2048]{0:T(1024)S(1)}, bf16[1,2048,1024]{1,2,0:T(8,128)(2,1)}) fusion(bf16[1,2048,1024]{1,2,0:T(8,128)(2,1)} %copy.1, bf16[1,6144,1024]{2,1,0:T(8,128)(2,1)} %all-gather.31.cloned.1.call-done, bf16[1,2048,6144]{2,1,0:T(8,128)(2,1)} %get-tuple-element.281), kind=kOutput, calls=%fused_computation.256 | convolution fusion | flops 25780287488 | bytes 46145536 | tf_op jit(solution)/vmap(jvp())/dot_general | solution.py:9
  516.0 35.1 %fusion.190 = f32[2048,6144]{1,0:T(8,128)} fusion(bf16[1,1024,6144]{2,1,0:T(8,128)(2,1)} %all-gather.33.cloned.1.call-done, bf16[1,2048,1024]{1,2,0:T(8,128)(2,1)} %fusion.208), kind=kOutput, calls=%fused_computation.237 | convolution fusion | flops 25769803776 | bytes 67108864 | tf_op jit(solution)/vmap(jvp())/dot_general | solution.py:20
  551.1 56.3 %fusion.174 = (bf16[1,2048,6144]{2,1,0:T(8,128)(2,1)}, f32[2048,6144]{1,0:T(8,128)}) fusion(f32[2048,6144]{1,0:T(8,128)} %fusion.190, bf16[1,1024,6144]{2,1,0:T(8,128)(2,1)} %all-gather.35.cloned.1.call-done, bf16[1,2048,1024]{1,2,0:T(8,128)(2,1)} %fusion.208), kind=kOutput, calls=%fused_computation.205 | convolution fusion | flops 25845301248 | bytes 142606336 | tf_op jit(solution)/vmap(jvp())/dot_general | solution.py:21
  607.4 30.2 %copy.4 = bf16[1,2048,6144]{1,2,0:T(8,128)(2,1)} copy(bf16[1,2048,6144]{2,1,0:T(8,128)(2,1)} %get-tuple-element.289) | data formatting | bytes 50331648
  637.6 322.1 %while.18 = (bf16[1,2048,6144]{1,2,0:T(8,128)(2,1)}, bf16[1,2048,1024]{2,1,0:T(8,128)(2,1)}, f32[384,1024]{1,0:T(8,128)S(1)}, f32[384,1024]{1,0:T(8,128)}, u32[]...) while((bf16[1,2048,6144]{1,2,0:T(8,128)(2,1)}, ...), condition=%wide.windowed_dot_general_cond_rs.4.clone, body=%wide.windowed_dot_general_body_rs.4.clone.sunk | while | flops 6457393152 | bytes 115343960 | solution.py:9
  665.0 32.4 %collective-permute-start.22 = (f32[384,1024]{1,0:T(8,128)}, f32[384,1024]{1,0:T(8,128)S(1)}, u32[]{:S(2)}, u32[]{:S(2)}) collective-permute-start(f32[384,1024]{1,0:T(8,128)} %get-tuple-element.543), channel_id=45, source_target_pairs={{0,1},{1,2},{2,3},{3,4},{4,5},{5,6},{6,7},{7,8},{8,9},{9,10},{10,1... | collective-permute-start | bytes 4718600 | tf_op jit(solution)/vmap(transpose(jvp()))/dot_general | solution.py:9
  799.2 17.5 collective-permute-start.20
  839.2 17.5 collective-permute-start.22
  880.6 18.1 collective-permute-start.20
  959.7 17.5 collective-permute-start.33
  977.2 58.3 %convert_multiply_fusion.3 = (bf16[1,2048,6144]{2,1,0:T(8,128)(2,1)}, bf16[1,2048,6144]{2,1,0:T(8,128)(2,1)}) fusion(f32[2048,6144]{1,0:T(8,128)} %fusion.190, bf16[1,2048,6144]{2,1,0:T(8,128)(2,1)} %copy.2, f32[2048,6144]{1,0:T(8,128)} %get-tuple-element.290), kind=kLoop, calls=%fused_computation.193 | loop fusion | flops 188743680 | bytes 176160768 | tf_op jit(solution)/vmap(transpose(jvp()))/mul | solution.py:22
  1035.5 34.3 %fusion.172 = bf16[2048,1024]{0,1:T(8,128)(2,1)} fusion(bf16[1,2048,6144]{2,1,0:T(8,128)(2,1)} %get-tuple-element.622, bf16[1,1024,6144]{2,1,0:T(8,128)(2,1)} %all-gather.33.cloned.1.call-done), kind=kOutput, calls=%fused_computation.202 | convolution fusion | flops 25769803776 | bytes 41943040 | tf_op jit(solution)/vmap(transpose(jvp()))/dot_general | solution.py:20
  1069.8 34.5 %fusion.209 = (f32[2048]{0:T(1024)S(1)}, bf16[2048,1024]{0,1:T(8,128)(2,1)S(1)}) fusion(bf16[1,2048,1024]{1,2,0:T(8,128)(2,1)S(1)} %copy-done.17, bf16[2048,1024]{0,1:T(8,128)(2,1)} %fusion.172, bf16[1,1024,6144]{2,1,0:T(8,128)(2,1)} %all-gather.35.cloned.1.call-done, bf16[1,2048,6144]{2,1,0:T(8,128)(2,1)} %get-tuple-element.694), kind=kOutput, calls=%fused_computation.258 | convolution fusion | flops 25780287488 | bytes 50339840 | tf_op jit(solution)/vmap(transpose(jvp()))/dot_general | solution.py:21
  1115.6 328.7 %while.19 = (bf16[1,2048,1024]{2,1,0:T(8,128)(2,1)}, bf16[1,2048,6144]{1,2,0:T(8,128)(2,1)}, f32[1024,384]{0,1:T(8,128)S(1)}, f32[1024,384]{0,1:T(8,128)}, u32[]...) while((bf16[1,2048,1024]{2,1,0:T(8,128)(2,1)}, ...), condition=%wide.windowed_dot_general_cond_rs.5.clone, body=%wide.windowed_dot_general_body_rs.5.clone.sunk | while | flops 6457393152 | bytes 115343960 | solution.py:9
  1143.5 32.4 %collective-permute-start.26 = (f32[1024,384]{0,1:T(8,128)}, f32[1024,384]{0,1:T(8,128)}, u32[]{:S(2)}, u32[]{:S(2)}) collective-permute-start(f32[1024,384]{0,1:T(8,128)} %get-tuple-element.552), channel_id=51, source_target_pairs={{0,1},{1,2},{2,3},{3,4},{4,5},{5,6},{6,7},{7,8},{8,9},{9,10},{10,1... | collective-permute-start | bytes 4718600 | tf_op jit(solution)/vmap(transpose(jvp()))/dot_general | solution.py:9
  1280.9 17.5 collective-permute-start.24
  1321.5 17.5 collective-permute-start.26
  1363.5 18.0 collective-permute-start.24
  1404.6 17.5 collective-permute-start.26
  1444.2 17.5 collective-permute-start.34
  1461.8 321.2 %while.16 = (bf16[1,2048,6144]{2,1,0:T(8,128)(2,1)}, bf16[1,2048,1024]{1,2,0:T(8,128)(2,1)}, f32[6144,64]{0,1:T(8,128)S(1)}, f32[6144,64]{0,1:T(8,128)}, u32[]{:...) while((bf16[1,2048,6144]{2,1,0:T(8,128)(2,1)}, ...), condition=%wide.windowed_dot_general_cond_rs.2.clone, body=%wide.windowed_dot_general_body_rs.2.clone.sunk | while | flops 6446907392 | bytes 115343960 | solution.py:21
  1488.7 32.4 %collective-permute-start.14 = (f32[6144,64]{0,1:T(8,128)}, f32[6144,64]{0,1:T(8,128)S(1)}, u32[]{:S(2)}, u32[]{:S(2)}) collective-permute-start(f32[6144,64]{0,1:T(8,128)} %get-tuple-element.525), channel_id=33, source_target_pairs={{0,1},{1,2},{2,3},{3,4},{4,5},{5,6},{6,7},{7,8},{8,9},{9,10},{10,1... | collective-permute-start | bytes 4718600 | tf_op jit(solution)/vmap(transpose(jvp()))/dot_general | solution.py:21
  1623.8 17.5 collective-permute-start.12
  1663.5 17.5 collective-permute-start.14
  1704.5 17.8 collective-permute-start.12
  1744.6 17.5 collective-permute-start.14
  1783.0 17.6 collective-permute-start.31
  1800.5 64.7 %convert_multiply_fusion.1 = (bf16[1,2048,6144]{2,1,0:T(8,128)(2,1)}, bf16[1,2048,6144]{2,1,0:T(8,128)(2,1)}) fusion(f32[2048,6144]{1,0:T(8,128)} %fusion.198, f32[2048,6144]{1,0:T(8,128)} %get-tuple-element.282, bf16[1,6144,1024]{2,1,0:T(8,128)(2,1)} %all-gather.31.cloned.1.call-done, bf16[1,2048,1024]{1,2,0:T(8,128)(2,1)} %fusion.211), kind=kOutput, calls=%fused_computation.191 | convolution fusion | flops 25971130368 | bytes 167772160 | tf_op jit(solution)/vmap(transpose(jvp()))/dot_general | solution.py:9
  1865.2 324.8 %while.17 = (bf16[1,2048,6144]{2,1,0:T(8,128)(2,1)}, bf16[1,2048,1024]{1,2,0:T(8,128)(2,1)}, f32[6144,64]{0,1:T(8,128)S(1)}, f32[6144,64]{0,1:T(8,128)}, u32[]{:...) while((bf16[1,2048,6144]{2,1,0:T(8,128)(2,1)}, ...), condition=%wide.windowed_dot_general_cond_rs.3.clone, body=%wide.windowed_dot_general_body_rs.3.clone.sunk | while | flops 6446907392 | bytes 115343960 | solution.py:21
  1892.9 32.4 %collective-permute-start.18 = (f32[6144,64]{0,1:T(8,128)}, f32[6144,64]{0,1:T(8,128)}, u32[]{:S(2)}, u32[]{:S(2)}) collective-permute-start(f32[6144,64]{0,1:T(8,128)} %get-tuple-element.534), channel_id=39, source_target_pairs={{0,1},{1,2},{2,3},{3,4},{4,5},{5,6},{6,7},{7,8},{8,9},{9,10},{10,1... | collective-permute-start | bytes 4718600 | tf_op jit(solution)/vmap(transpose(jvp()))/dot_general | solution.py:21
  2028.9 17.5 collective-permute-start.16
  2069.1 17.5 collective-permute-start.18
  2110.6 17.8 collective-permute-start.16
  2151.1 17.5 collective-permute-start.18
  2191.2 326.1 %while.14 = (bf16[1,2048,6144]{2,1,0:T(8,128)(2,1)}, bf16[1,2048,1024]{1,2,0:T(8,128)(2,1)}, f32[6144,64]{0,1:T(8,128)S(1)}, f32[6144,64]{0,1:T(8,128)}, u32[]{:...) while((bf16[1,2048,6144]{2,1,0:T(8,128)(2,1)}, ...), condition=%wide.windowed_dot_general_cond_rs.clone, body=%wide.windowed_dot_general_body_rs.clone.sunk | while | flops 6446907392 | bytes 115343960 | solution.py:20
  2192.4 17.5 collective-permute-start.4
  2232.7 17.4 collective-permute-start.6
  2274.2 17.6 collective-permute-start.4
  2314.5 17.4 collective-permute-start.6
  2356.1 17.5 collective-permute-start.4
  2396.3 17.4 collective-permute-start.6
  2437.8 17.8 collective-permute-start.4
  2478.4 17.4 collective-permute-start.6
  2518.4 322.3 %while.15 = (bf16[1,2048,6144]{2,1,0:T(8,128)(2,1)}, bf16[1,2048,1024]{1,2,0:T(8,128)(2,1)}, f32[6144,64]{0,1:T(8,128)S(1)}, f32[6144,64]{0,1:T(8,128)}, u32[]{:...) while((bf16[1,2048,6144]{2,1,0:T(8,128)(2,1)}, ...), condition=%wide.windowed_dot_general_cond_rs.1.clone, body=%wide.windowed_dot_general_body_rs.1.clone.sunk | while | flops 6446907392 | bytes 115343960 | solution.py:20
  2519.9 17.5 collective-permute-start.8
  2559.6 17.5 collective-permute-start.10
  2600.7 17.6 collective-permute-start.8
  2640.5 17.5 collective-permute-start.10
  2681.5 17.5 collective-permute-start.8
  2721.2 17.5 collective-permute-start.10
  2762.3 17.8 collective-permute-start.8
  2802.4 17.5 collective-permute-start.10
  2840.8 17.5 collective-permute-start.32
  2858.3 34.1 %fusion.168 = bf16[2048,1024]{0,1:T(8,128)(2,1)} fusion(bf16[1,2048,6144]{2,1,0:T(8,128)(2,1)} %get-tuple-element.808, bf16[1,1024,6144]{2,1,0:T(8,128)(2,1)} %all-gather.27.cloned.1.call-done), kind=kOutput, calls=%fused_computation.198 | convolution fusion | flops 25769803776 | bytes 41943040 | tf_op jit(solution)/vmap(transpose(jvp()))/dot_general | solution.py:20
  2892.4 35.5 %fusion.206 = (f32[2048]{0:T(1024)S(1)}, bf16[2048,1024]{0,1:T(8,128)(2,1)}) fusion(bf16[1,2048,1024]{1,2,0:T(8,128)(2,1)S(1)} %copy-done, bf16[2048,1024]{0,1:T(8,128)(2,1)} %fusion.168, bf16[1,1024,6144]{2,1,0:T(8,128)(2,1)} %all-gather.29.cloned.1.call-done, bf16[1,2048,6144]{2,1,0:T(8,128)(2,1)} %get-tuple-element.807), kind=kOutput, calls=%fused_computation.255 | convolution fusion | flops 25780287488 | bytes 50339840 | tf_op jit(solution)/vmap(transpose(jvp()))/dot_general | solution.py:21
  (476 shorter events, 1551.3 us)
Async XLA Ops:
  7.2 331.3 %all-gather.27.cloned.1.call-start = ((), (), s32[]{:S(2)}) async-start(), calls=%async_computation | async-start | bytes 13369344 | tf_op jit(solution)/vmap(jvp())/squeeze | solution.py:27
  10.1 363.8 %all-gather.29.cloned.1.call-start = ((), (), s32[]{:S(2)}) async-start(), calls=%async_computation.1 | async-start | bytes 13369344 | tf_op jit(solution)/vmap(jvp())/squeeze | solution.py:27
  11.5 451.2 %all-gather.31.cloned.1.call-start = ((), (), s32[]{:S(2)}) async-start(), calls=%async_computation.2 | async-start | bytes 13369344 | tf_op jit(solution)/vmap(jvp())/squeeze | solution.py:27
  12.8 503.2 %all-gather.33.cloned.1.call-start = ((), (), s32[]{:S(2)}) async-start(), calls=%async_computation.3 | async-start | bytes 13369344 | tf_op jit(solution)/vmap(jvp())/squeeze | solution.py:27
  13.4 537.7 %all-gather.35.cloned.1.call-start = ((), (), s32[]{:S(2)}) async-start(), calls=%async_computation.4 | async-start | bytes 13369344 | tf_op jit(solution)/vmap(jvp())/squeeze | solution.py:27
  45.1 23.9 collective-permute-start
  69.1 29.9 %collective-permute-start.1 = (bf16[1,384,1024]{2,1,0:T(8,128)(2,1)}, bf16[1,384,1024]{2,1,0:T(8,128)(2,1)}, u32[]{:S(2)}, u32[]{:S(2)}) collective-permute-start(bf16[1,384,1024]{2,1,0:T(8,128)(2,1)} %collective-permute-done), channel_id=9, source_target_pairs={{0,15},{1,0},{2,1},{3,2},{4,3},{5,4},{6,5},{7,6},{8,7},{9,8},{10,9... | collective-permute-start | bytes 2359304 | tf_op jit(solution)/vmap(transpose(jvp()))/dot_general | solution.py:9
  99.0 30.5 %collective-permute-start = (bf16[1,384,1024]{2,1,0:T(8,128)(2,1)}, bf16[1,384,1024]{2,1,0:T(8,128)(2,1)}, u32[]{:S(2)}, u32[]{:S(2)}) collective-permute-start(bf16[1,384,1024]{2,1,0:T(8,128)(2,1)} %get-tuple-element.567), channel_id=7, source_target_pairs={{0,15},{1,0},{2,1},{3,2},{4,3},{5,4},{6,5},{7,6},{8,7},{9,8},{10,9... | collective-permute-start | bytes 2359304 | tf_op jit(solution)/vmap(transpose(jvp()))/dot_general | solution.py:9
  99.0 32.3 %collective-permute-start.2 = (bf16[1,384,1024]{2,1,0:T(8,128)(2,1)}, bf16[1,384,1024]{2,1,0:T(8,128)(2,1)}, u32[]{:S(2)}, u32[]{:S(2)}) collective-permute-start(bf16[1,384,1024]{2,1,0:T(8,128)(2,1)} %get-tuple-element.569), channel_id=8, source_target_pairs={{0,1},{1,2},{2,3},{3,4},{4,5},{5,6},{6,7},{7,8},{8,9},{9,10},{10,1... | collective-permute-start | bytes 2359304 | tf_op jit(solution)/vmap(transpose(jvp()))/dot_general | solution.py:9
  129.5 26.4 collective-permute-start.1
  137.4 26.2 collective-permute-start.3
  163.6 33.6 %collective-permute-start = (bf16[1,384,1024]{2,1,0:T(8,128)(2,1)}, bf16[1,384,1024]{2,1,0:T(8,128)(2,1)}, u32[]{:S(2)}, u32[]{:S(2)}) collective-permute-start(bf16[1,384,1024]{2,1,0:T(8,128)(2,1)} %get-tuple-element.567), channel_id=7, source_target_pairs={{0,15},{1,0},{2,1},{3,2},{4,3},{5,4},{6,5},{7,6},{8,7},{9,8},{10,9... | collective-permute-start | bytes 2359304 | tf_op jit(solution)/vmap(transpose(jvp()))/dot_general | solution.py:9
  163.6 33.6 %collective-permute-start.2 = (bf16[1,384,1024]{2,1,0:T(8,128)(2,1)}, bf16[1,384,1024]{2,1,0:T(8,128)(2,1)}, u32[]{:S(2)}, u32[]{:S(2)}) collective-permute-start(bf16[1,384,1024]{2,1,0:T(8,128)(2,1)} %get-tuple-element.569), channel_id=8, source_target_pairs={{0,1},{1,2},{2,3},{3,4},{4,5},{5,6},{6,7},{7,8},{8,9},{9,10},{10,1... | collective-permute-start | bytes 2359304 | tf_op jit(solution)/vmap(transpose(jvp()))/dot_general | solution.py:9
  197.2 23.4 collective-permute-start.1
  225.7 24.1 collective-permute-start
  225.7 39.3 %collective-permute-start.2 = (bf16[1,384,1024]{2,1,0:T(8,128)(2,1)}, bf16[1,384,1024]{2,1,0:T(8,128)(2,1)}, u32[]{:S(2)}, u32[]{:S(2)}) collective-permute-start(bf16[1,384,1024]{2,1,0:T(8,128)(2,1)} %get-tuple-element.569), channel_id=8, source_target_pairs={{0,1},{1,2},{2,3},{3,4},{4,5},{5,6},{6,7},{7,8},{8,9},{9,10},{10,1... | collective-permute-start | bytes 2359304 | tf_op jit(solution)/vmap(transpose(jvp()))/dot_general | solution.py:9
  249.8 30.4 %collective-permute-start.1 = (bf16[1,384,1024]{2,1,0:T(8,128)(2,1)}, bf16[1,384,1024]{2,1,0:T(8,128)(2,1)}, u32[]{:S(2)}, u32[]{:S(2)}) collective-permute-start(bf16[1,384,1024]{2,1,0:T(8,128)(2,1)} %collective-permute-done), channel_id=9, source_target_pairs={{0,15},{1,0},{2,1},{3,2},{4,3},{5,4},{6,5},{7,6},{8,7},{9,8},{10,9... | collective-permute-start | bytes 2359304 | tf_op jit(solution)/vmap(transpose(jvp()))/dot_general | solution.py:9
  271.1 34.7 %collective-permute-start.3 = (bf16[1,384,1024]{2,1,0:T(8,128)(2,1)}, bf16[1,384,1024]{2,1,0:T(8,128)(2,1)}, u32[]{:S(2)}, u32[]{:S(2)}) collective-permute-start(bf16[1,384,1024]{2,1,0:T(8,128)(2,1)} %collective-permute-done.2), channel_id=10, source_target_pairs={{0,1},{1,2},{2,3},{3,4},{4,5},{5,6},{6,7},{7,8},{8,9},{9,10},{10,1... | collective-permute-start | bytes 2359304 | tf_op jit(solution)/vmap(transpose(jvp()))/dot_general | solution.py:9
  665.0 38.5 %collective-permute-start.22 = (f32[384,1024]{1,0:T(8,128)}, f32[384,1024]{1,0:T(8,128)S(1)}, u32[]{:S(2)}, u32[]{:S(2)}) collective-permute-start(f32[384,1024]{1,0:T(8,128)} %get-tuple-element.543), channel_id=45, source_target_pairs={{0,1},{1,2},{2,3},{3,4},{4,5},{5,6},{6,7},{7,8},{8,9},{9,10},{10,1... | collective-permute-start | bytes 4718600 | tf_op jit(solution)/vmap(transpose(jvp()))/dot_general | solution.py:9
  799.2 24.9 collective-permute-start.20
  839.2 23.6 collective-permute-start.22
  880.6 25.6 collective-permute-start.20
  921.2 23.4 collective-permute-start.22
  959.7 1987.2 %collective-permute-start.33 = (f32[384,1024]{1,0:T(8,128)}, f32[384,1024]{1,0:T(8,128)}, u32[]{:S(2)}, u32[]{:S(2)}) collective-permute-start(f32[384,1024]{1,0:T(8,128)} %get-tuple-element.52), channel_id=46, source_target_pairs={{0,1},{1,2},{2,3},{3,4},{4,5},{5,6},{6,7},{7,8},{8,9},{9,10},{10,1... | collective-permute-start | bytes 4718600 | tf_op jit(solution)/vmap(transpose(jvp()))/dot_general | solution.py:9
  1143.5 38.5 %collective-permute-start.26 = (f32[1024,384]{0,1:T(8,128)}, f32[1024,384]{0,1:T(8,128)}, u32[]{:S(2)}, u32[]{:S(2)}) collective-permute-start(f32[1024,384]{0,1:T(8,128)} %get-tuple-element.552), channel_id=51, source_target_pairs={{0,1},{1,2},{2,3},{3,4},{4,5},{5,6},{6,7},{7,8},{8,9},{9,10},{10,1... | collective-permute-start | bytes 4718600 | tf_op jit(solution)/vmap(transpose(jvp()))/dot_general | solution.py:9
  1200.5 23.6 collective-permute-start.24
  1280.9 24.9 collective-permute-start.24
  1321.5 23.6 collective-permute-start.26
  1363.5 25.4 collective-permute-start.24
  1404.6 23.6 collective-permute-start.26
  1444.2 1504.4 %collective-permute-start.34 = (f32[1024,384]{0,1:T(8,128)}, f32[1024,384]{0,1:T(8,128)}, u32[]{:S(2)}, u32[]{:S(2)}) collective-permute-start(f32[1024,384]{0,1:T(8,128)} %get-tuple-element.54), channel_id=52, source_target_pairs={{0,1},{1,2},{2,3},{3,4},{4,5},{5,6},{6,7},{7,8},{8,9},{9,10},{10,1... | collective-permute-start | bytes 4718600 | tf_op jit(solution)/vmap(transpose(jvp()))/dot_general | solution.py:9
  1488.7 42.5 %collective-permute-start.14 = (f32[6144,64]{0,1:T(8,128)}, f32[6144,64]{0,1:T(8,128)S(1)}, u32[]{:S(2)}, u32[]{:S(2)}) collective-permute-start(f32[6144,64]{0,1:T(8,128)} %get-tuple-element.525), channel_id=33, source_target_pairs={{0,1},{1,2},{2,3},{3,4},{4,5},{5,6},{6,7},{7,8},{8,9},{9,10},{10,1... | collective-permute-start | bytes 4718600 | tf_op jit(solution)/vmap(transpose(jvp()))/dot_general | solution.py:21
  1544.7 27.6 collective-permute-start.12
  1583.1 27.2 collective-permute-start.14
  1623.8 28.9 collective-permute-start.12
  1663.5 27.6 collective-permute-start.14
  1704.5 29.2 collective-permute-start.12
  1744.6 27.6 collective-permute-start.14
  1783.0 1160.1 %collective-permute-start.31 = (f32[6144,64]{0,1:T(8,128)}, f32[6144,64]{0,1:T(8,128)}, u32[]{:S(2)}, u32[]{:S(2)}) collective-permute-start(f32[6144,64]{0,1:T(8,128)} %get-tuple-element.48), channel_id=34, source_target_pairs={{0,1},{1,2},{2,3},{3,4},{4,5},{5,6},{6,7},{7,8},{8,9},{9,10},{10,1... | collective-permute-start | bytes 4718600 | tf_op jit(solution)/vmap(transpose(jvp()))/dot_general | solution.py:21
  1892.9 42.5 %collective-permute-start.18 = (f32[6144,64]{0,1:T(8,128)}, f32[6144,64]{0,1:T(8,128)}, u32[]{:S(2)}, u32[]{:S(2)}) collective-permute-start(f32[6144,64]{0,1:T(8,128)} %get-tuple-element.534), channel_id=39, source_target_pairs={{0,1},{1,2},{2,3},{3,4},{4,5},{5,6},{6,7},{7,8},{8,9},{9,10},{10,1... | collective-permute-start | bytes 4718600 | tf_op jit(solution)/vmap(transpose(jvp()))/dot_general | solution.py:21
  1949.4 27.6 collective-permute-start.16
  1988.3 26.7 collective-permute-start.18
  2028.9 28.9 collective-permute-start.16
  2069.1 27.6 collective-permute-start.18
  2110.6 29.2 collective-permute-start.16
  2151.1 27.6 collective-permute-start.18
  2192.4 29.0 collective-permute-start.4
  2232.7 27.6 collective-permute-start.6
  2274.2 29.0 collective-permute-start.4
  2314.5 27.6 collective-permute-start.6
  2356.1 29.0 collective-permute-start.4
  2396.3 27.6 collective-permute-start.6
  2437.8 29.3 collective-permute-start.4
  2478.4 27.6 collective-permute-start.6
  2519.9 28.9 collective-permute-start.8
  2559.6 27.7 collective-permute-start.10
  2600.7 29.0 collective-permute-start.8
  2640.5 27.6 collective-permute-start.10
  2681.5 28.9 collective-permute-start.8
  2721.2 27.6 collective-permute-start.10
  2762.3 29.2 collective-permute-start.8
  2802.4 27.7 collective-permute-start.10
  2840.8 104.5 %collective-permute-start.32 = (f32[6144,64]{0,1:T(8,128)}, f32[6144,64]{0,1:T(8,128)}, u32[]{:S(2)}, u32[]{:S(2)}) collective-permute-start(f32[6144,64]{0,1:T(8,128)} %get-tuple-element.50), channel_id=40, source_target_pairs={{0,1},{1,2},{2,3},{3,4},{4,5},{5,6},{6,7},{7,8},{8,9},{9,10},{10,1... | collective-permute-start | bytes 4718600 | tf_op jit(solution)/vmap(transpose(jvp()))/dot_general | solution.py:21
  2943.1 36.0 %collective-permute-start.30 = (f32[6144,64]{0,1:T(8,128)}, f32[6144,64]{0,1:T(8,128)S(1)}, u32[]{:S(2)}, u32[]{:S(2)}) collective-permute-start(f32[6144,64]{0,1:T(8,128)} %get-tuple-element.46), channel_id=28, source_target_pairs={{0,1},{1,2},{2,3},{3,4},{4,5},{5,6},{6,7},{7,8},{8,9},{9,10},{10,1... | collective-permute-start | bytes 4718600 | tf_op jit(solution)/vmap(transpose(jvp()))/dot_general | solution.py:20
  (89 other events, 2690.8 us)
Sparse Core Ops, SparseCore 0:
  10.3 94.6 all-gather.26
  107.2 96.7 all-gather.28
  206.2 109.6 all-gather.30
  318.0 62.2 all-gather.32
  382.4 62.2 all-gather.34
where the time goes:
time: 3000 us; the launch traced here: 2990 us
  starting transfers between devices  1040 us (35%)
  matrix products  904 us (30%)
  waiting for transfers between devices  528 us (18%)
  other arithmetic  341 us (11%)
  local copies, waits for them, and re-layouts  160 us (5%)
    dot_general x51, starting transfers between devices, matmul(): jnp.dot(a, w, preferred_element_type=jnp.float32).astype(jnp.bfloat16)  441 us
    dot_general x20, matrix products, layer(): up = jnp.dot(a, w['w_up'], preferred_element_type=jnp.float32)  344 us
    dot_general x34, starting transfers between devices, layer(): up = jnp.dot(a, w['w_up'], preferred_element_type=jnp.float32)  314 us
    dot_general x20, matrix products, layer(): gate = jnp.dot(a, w['w_gate'], preferred_element_type=jnp.float32)  302 us
    dot_general x34, starting transfers between devices, layer(): gate = jnp.dot(a, w['w_gate'], preferred_element_type=jnp.float32)  283 us
    dot_general x26, matrix products, matmul(): jnp.dot(a, w, preferred_element_type=jnp.float32).astype(jnp.bfloat16)  258 us
    dot_general x51, waiting for transfers between devices, matmul(): jnp.dot(a, w, preferred_element_type=jnp.float32).astype(jnp.bfloat16)  252 us
    dot_general x34, waiting for transfers between devices, layer(): gate = jnp.dot(a, w['w_gate'], preferred_element_type=jnp.float32)  150 us
  transfers between devices with their start and end apart: 124, of which 60 were waited for; matrix products, arithmetic and copies ran while one was open for 43% of the time, Pallas kernels for 0%

commit v1 on v0

v1 whole, which is shorter than its diff:
```python
import jax
import jax.numpy as jnp
from jax import lax
from jax.sharding import PartitionSpec as P

LAYERS = 2
BF, F32 = jnp.bfloat16, jnp.float32


def dot(a, b, dims):
    return lax.dot_general(a, b, (dims, ((), ())), preferred_element_type=F32)


NN, NT, TN = ((1,), (0,)), ((1,), (1,)), ((0,), (0,))


def scale_of(h):
    wide = h.astype(F32)
    return lax.rsqrt(jnp.mean(wide**2, -1, keepdims=True) + 1e-6)


def norm_back(h, scale, da):
    wide = h.astype(F32)
    inner = jnp.mean(wide * da, -1, keepdims=True)
    return scale * da - wide * (scale**3 * inner)


def solution(mesh):
    def body(x, dy, w_gate, w_up, w_down):
        x, dy = x[0], dy[0]
        gather = lambda w: lax.all_gather(w, "dp", axis=0, tiled=True)
        scatter = lambda g: lax.psum_scatter(g, "dp", scatter_dimension=0, tiled=True)
        wg, wu, wd = ([gather(w[n]) for n in range(LAYERS)] for w in (w_gate, w_up, w_down))
        h, kept = x, []
        for n in range(LAYERS):
            scale = scale_of(h)
            a = (h.astype(F32) * scale).astype(BF)
            gate, up = dot(a, wg[n], NN), dot(a, wu[n], NN)
            hid = (jax.nn.silu(gate) * up).astype(BF)
            kept.append((h, scale, a, gate, up, hid))
            if n < LAYERS - 1:
                h = h + dot(hid, wd[n], NN).astype(BF)
        dh, grads = dy, [None] * LAYERS
        for n in reversed(range(LAYERS)):
            h, scale, a, gate, up, hid = kept[n]
            dwd = scatter(dot(hid, dh, TN).astype(BF))
            dhid = dot(dh, wd[n], NT).astype(BF).astype(F32)
            sig = jax.nn.sigmoid(gate)
            silu = gate * sig
            dgate = (dhid * up * (sig + silu * (1 - sig))).astype(BF)
            dup = (dhid * silu).astype(BF)
            dwg = scatter(dot(a, dgate, TN).astype(BF))
            dwu = scatter(dot(a, dup, TN).astype(BF))
            da = dot(dgate, wg[n], NT) + dot(dup, wu[n], NT)
            dh = (dh.astype(F32) + norm_back(h, scale, da)).astype(BF)
            grads[n] = (dwg, dwu, dwd)
        return (dh[None], *(jnp.stack([g[k] for g in grads]) for k in range(3)))

    rows = P(None, "dp", None)
    data = P(("rep", "dp"), None, None)
    return jax.shard_map(body, mesh=mesh, in_specs=(data, data, rows, rows, rows), out_specs=(data, rows, rows, rows), check_vma=False)
```

time: 3000 us -> 1170 us (0.39)
  starting transfers between devices: 1040 us -> 0.49 us
  other arithmetic: 341 us -> 22.2 us
  matrix products: 904 us -> 710 us
  waiting for transfers between devices: 528 us -> 381 us
  local copies, waits for them, and re-layouts: 160 us -> 31.2 us
    dot_general x119 -> x0, starting transfers between devices: 1040 us -> none  [the longest x51 441 us: matmul(): jnp.dot(a, w, preferred_element_type=jnp.float32).astype(jnp.bfloat16)]
    dot_general x119 -> x0, waiting for transfers between devices: 528 us -> none  [the longest x51 252 us: matmul(): jnp.dot(a, w, preferred_element_type=jnp.float32).astype(jnp.bfloat16)]
    dot_general x96 -> x0, other arithmetic: 246 us -> none
    reduce_scatter x0 -> x6, waiting for transfers between devices: none -> 221 us  [body(): lax.psum_scatter(g, 'dp', scatter_dimension=0, tiled=True)]
    dot_general x66 -> x17, matrix products: 904 us -> 710 us  [dot(): return lax.dot_general(a, b, (dims, ((), ())), preferred_element_type=F32)]
    all_gather x0 -> x6, waiting for transfers between devices: none -> 158 us  [body(): gather = lambda w: lax.all_gather(w, 'dp', axis=0, tiled=True)]
    unnamed x64 -> x35, local copies, waits for them, and re-layouts: 93.1 us -> 23.2 us
    dot_general x18 -> x0, local copies, waits for them, and re-layouts: 61.7 us -> none  [matmul(): jnp.dot(a, w, preferred_element_type=jnp.float32).astype(jnp.bfloat16)]
  transfers between devices with their start and end apart: 124 -> 12, of which waited for: 60 -> 9; matrix products, arithmetic and copies ran while one was open for 43% -> 49% of each run, Pallas kernels for 0% -> 0%
where the time goes in v1:
time: 1170 us; the launch traced here: 1160 us
  matrix products  710 us (61%)
  waiting for transfers between devices  381 us (33%)
  local copies, waits for them, and re-layouts  31.2 us (3%)
  other arithmetic  22.2 us (2%)
  between operations  14.5 us (1%)
    dot_general x17, matrix products, dot(): return lax.dot_general(a, b, (dims, ((), ())), preferred_element_type=F32)  710 us
    reduce_scatter x6, waiting for transfers between devices, body(): lax.psum_scatter(g, 'dp', scatter_dimension=0, tiled=True)  221 us
    all_gather x6, waiting for transfers between devices, body(): gather = lambda w: lax.all_gather(w, 'dp', axis=0, tiled=True)  158 us
  transfers between devices with their start and end apart: 12, of which 9 were waited for; matrix products, arithmetic and copies ran while one was open for 49% of the time, Pallas kernels for 0%

profile of v1, /device:TPU:0, one launch (start us, length us, event | category | flops | bytes accessed | tf_op | source)
XLA Modules:
  0.0 1159.6 jit_solution(890703796567197510)
XLA Ops:
  7.2 0.0 all-gather.13.cloned.1.call-start
  7.2 2.7 fusion.72
  9.9 0.0 all-gather.13.cloned.1.call-update
  9.9 0.0 all-gather.15.cloned.1.call-start
  10.0 2.7 fusion.74
  12.6 0.0 all-gather.15.cloned.1.call-update
  12.6 0.0 all-gather.17.cloned.1.call-start
  12.7 2.7 fusion.73
  15.4 0.0 all-gather.17.cloned.1.call-update
  15.4 0.0 all-gather.19.cloned.1.call-start
  15.5 0.5 all-gather.19.cloned.1.call-update
  16.0 0.0 all-gather.23.cloned.1.call-start
  16.0 0.5 all-gather.23.cloned.1.call-update
  16.6 0.0 all-gather.21.cloned.1.call-start
  16.6 0.5 all-gather.21.cloned.1.call-update
  17.1 0.0 reduce-scatter.15.cloned.1.call-start
  17.2 6.4 copy.10
  23.6 3.1 fusion.30
  26.7 0.6 copy-done.5
  27.3 6.5 copy.9
  33.8 41.5 %all-gather.13.cloned.1.call-done = bf16[1,1024,6144]{2,1,0:T(8,128)(2,1)} async-done(((bf16[1,64,6144]{2,1,0:T(8,128)(2,1)}), bf16[1,1024,6144]{2,1,0:T(8,128)(2,1)}) %all-gather.13.cloned.1.call-update) | async-done | bytes 12582928 | tf_op jit(solution)/shard_map/all_gather | solution.py:31
  75.4 34.8 %fusion.27 = f32[2048,6144]{1,0:T(8,128)} fusion(bf16[1,1024,6144]{2,1,0:T(8,128)(2,1)} %all-gather.13.cloned.1.call-done, bf16[1,2048,1024]{1,2,0:T(8,128)(2,1)} %copy.10, f32[2048]{0:T(1024)S(1)} %add_rsqrt_fusion.1), kind=kOutput, calls=%fused_computation.45 | convolution fusion | flops 25776095232 | bytes 67117056 | tf_op jit(solution)/shard_map/dot_general | solution.py:11
  110.2 30.3 %all-gather.15.cloned.1.call-done = bf16[1,1024,6144]{2,1,0:T(8,128)(2,1)} async-done(((bf16[1,64,6144]{2,1,0:T(8,128)(2,1)}), bf16[1,1024,6144]{2,1,0:T(8,128)(2,1)}) %all-gather.15.cloned.1.call-update) | async-done | bytes 12582928 | tf_op jit(solution)/shard_map/all_gather | solution.py:31
  140.5 56.7 %multiply_convert_fusion.1 = (bf16[2048,6144]{1,0:T(8,128)(2,1)}, f32[2048,6144]{1,0:T(8,128)}) fusion(f32[2048,6144]{1,0:T(8,128)} %fusion.27, bf16[1,1024,6144]{2,1,0:T(8,128)(2,1)} %all-gather.15.cloned.1.call-done, bf16[1,2048,1024]{1,2,0:T(8,128)(2,1)} %copy.10, f32[2048]{0:T(1024)S(1)} %add_rsqrt_fusion.1), kind=kOutput, calls=%fused_computation.12 | convolution fusion | flops 25851592704 | bytes 142614528 | tf_op jit(solution)/shard_map/dot_general | solution.py:11
  197.2 7.9 all-gather.17.cloned.1.call-done
  205.0 46.6 %fusion.36 = (f32[2048]{0:T(1024)S(1)}, bf16[2048,1024]{0,1:T(8,128)(2,1)}) fusion(bf16[2048,6144]{1,0:T(8,128)(2,1)} %get-tuple-element.14, bf16[1,6144,1024]{2,1,0:T(8,128)(2,1)} %all-gather.17.cloned.1.call-done, bf16[1,2048,1024]{1,2,0:T(8,128)(2,1)} %copy.10), kind=kOutput, calls=%fused_computation.59 | convolution fusion | flops 25780287488 | bytes 46145536 | tf_op jit(solution)/shard_map/dot_general | solution.py:11
  251.7 17.8 %all-gather.19.cloned.1.call-done = bf16[1,6144,1024]{2,1,0:T(8,128)(2,1)} async-done(((bf16[1,384,1024]{2,1,0:T(8,128)(2,1)}), bf16[1,6144,1024]{2,1,0:T(8,128)(2,1)}) %all-gather.19.cloned.1.call-update) | async-done | bytes 12582928 | tf_op jit(solution)/shard_map/all_gather | solution.py:31
  269.4 34.1 %convolution_convert_fusion.1 = bf16[2048,6144]{1,0:T(8,128)(2,1)} fusion(bf16[1,6144,1024]{2,1,0:T(8,128)(2,1)} %all-gather.19.cloned.1.call-done, bf16[1,2048,1024]{2,1,0:T(8,128)(2,1)} %param.6), kind=kOutput, calls=%fused_computation.18 | convolution fusion | flops 25782386688 | bytes 41943040 | tf_op jit(solution)/shard_map/dot_general | solution.py:11
  303.6 30.8 %all-gather.23.cloned.1.call-done = bf16[1,1024,6144]{2,1,0:T(8,128)(2,1)} async-done(((bf16[1,64,6144]{2,1,0:T(8,128)(2,1)}), bf16[1,1024,6144]{2,1,0:T(8,128)(2,1)}) %all-gather.23.cloned.1.call-update) | async-done | bytes 12582928 | tf_op jit(solution)/shard_map/all_gather | solution.py:31
  334.4 35.1 %fusion.11 = f32[2048,6144]{1,0:T(8,128)} fusion(bf16[1,1024,6144]{2,1,0:T(8,128)(2,1)} %all-gather.23.cloned.1.call-done, bf16[2048,1024]{0,1:T(8,128)(2,1)} %get-tuple-element.17, f32[2048]{0:T(1024)S(1)} %add_rsqrt_fusion), kind=kOutput, calls=%fused_computation.29 | convolution fusion | flops 25776095232 | bytes 67117056 | tf_op jit(solution)/shard_map/dot_general | solution.py:11
  369.5 29.9 %all-gather.21.cloned.1.call-done = bf16[1,1024,6144]{2,1,0:T(8,128)(2,1)} async-done(((bf16[1,64,6144]{2,1,0:T(8,128)(2,1)}), bf16[1,1024,6144]{2,1,0:T(8,128)(2,1)}) %all-gather.21.cloned.1.call-update) | async-done | bytes 12582928 | tf_op jit(solution)/shard_map/all_gather | solution.py:31
  399.4 68.0 %fusion.1 = (bf16[2048,6144]{1,0:T(8,128)(2,1)}, f32[2048,6144]{1,0:T(8,128)}) fusion(bf16[2048,6144]{1,0:T(8,128)(2,1)} %convolution_convert_fusion.1, f32[2048,6144]{1,0:T(8,128)} %fusion.11, bf16[1,1024,6144]{2,1,0:T(8,128)(2,1)} %all-gather.21.cloned.1.call-done, bf16[2048,1024]{0,1:T(8,128)(2,1)} %get-tuple-element.17, f32[2048]{0:T(1024)S(1)} %add_rsqrt_fusion), kind=kOutput, calls=%fused_computation.5 | convolution fusion | flops 25914507264 | bytes 167780352 | tf_op jit(solution)/shard_map/dot_general | solution.py:11
  467.4 34.9 %fusion.9 = f32[2048,1024]{0,1:T(8,128)} fusion(bf16[2048,6144]{1,0:T(8,128)(2,1)} %get-tuple-element.18, bf16[1,1024,6144]{2,1,0:T(8,128)(2,1)} %all-gather.23.cloned.1.call-done), kind=kOutput, calls=%fused_computation.27 | convolution fusion | flops 25769803776 | bytes 46137344 | tf_op jit(solution)/shard_map/dot_general | solution.py:11
  502.2 42.7 %fusion.38 = (f32[2048]{0:T(1024)S(1)}, f32[2048,1024]{0,1:T(8,128)}) fusion(bf16[2048,1024]{0,1:T(8,128)(2,1)S(1)} %copy-done.4, f32[2048,1024]{0,1:T(8,128)} %fusion.9, bf16[1,1024,6144]{2,1,0:T(8,128)(2,1)} %all-gather.21.cloned.1.call-done, bf16[2048,6144]{1,0:T(8,128)(2,1)} %convolution_convert_fusion.1, f32[2048,6144]{1,0:T(8,128)} %fusion.11), kind=kOutput, calls=%fused_computation.61 | convolution fusion | flops 25866270720 | bytes 109060096 | tf_op jit(solution)/shard_map/dot_general | solution.py:11
  545.0 5.0 fusion.41
  549.9 1.9 copy-done.2
  551.9 32.3 %convolution_convert_fusion.2 = bf16[6144,1024]{1,0:T(8,128)(2,1)} fusion(bf16[2048,6144]{1,0:T(8,128)(2,1)} %get-tuple-element.14, bf16[2048,1024]{0,1:T(8,128)(2,1)S(1)} %fusion.41), kind=kOutput, calls=%fused_computation.48 | convolution fusion | flops 25776095232 | bytes 41943040 | tf_op jit(solution)/shard_map/dot_general | solution.py:11
  584.1 0.0 reduce-scatter.15.cloned.1.call-update
  584.2 0.0 reduce-scatter.17.cloned.1.call-start
  584.2 42.7 %fusion.29 = bf16[6144,1024]{1,0:T(8,128)(2,1)} fusion(f32[2048,6144]{1,0:T(8,128)} %get-tuple-element.19, bf16[1,2048,1024]{2,1,0:T(8,128)(2,1)} %param.6, f32[2048,6144]{1,0:T(8,128)} %fusion.11), kind=kOutput, calls=%fused_computation.47 | convolution fusion | flops 25851592704 | bytes 117440512 | tf_op jit(solution)/shard_map/dot_general | solution.py:11
  627.0 0.0 reduce-scatter.11.cloned.1.call-start
  627.0 66.8 %fusion.4 = (bf16[2048,6144]{1,0:T(8,128)(2,1)}, bf16[2048,6144]{1,0:T(8,128)(2,1)}) fusion(f32[2048,6144]{1,0:T(8,128)} %get-tuple-element.15, f32[2048,6144]{1,0:T(8,128)} %fusion.27, bf16[2048,1024]{0,1:T(8,128)(2,1)} %copy-done.2, bf16[1,6144,1024]{2,1,0:T(8,128)(2,1)} %all-gather.17.cloned.1.call-done), kind=kOutput, calls=%fused_computation.8 | convolution fusion | flops 25920798720 | bytes 167772160 | tf_op jit(solution)/shard_map/dot_general | solution.py:11
  693.8 38.3 %convolution_convert_fusion.4 = bf16[1024,6144]{1,0:T(8,128)(2,1)} fusion(bf16[1,2048,1024]{1,2,0:T(8,128)(2,1)} %copy.10, f32[2048]{0:T(1024)S(1)} %copy-done.8, bf16[2048,6144]{1,0:T(8,128)(2,1)} %get-tuple-element.23, f32[2048,6144]{1,0:T(8,128)} %fusion.27), kind=kOutput, calls=%fused_computation.50 | convolution fusion | flops 25870467072 | bytes 92282880 | tf_op jit(solution)/shard_map/dot_general | solution.py:11
  732.1 0.0 reduce-scatter.11.cloned.1.call-update
  732.1 0.0 reduce-scatter.13.cloned.1.call-start
  732.2 0.6 copy-done.13
  732.8 38.5 %convolution_convert_fusion.3 = bf16[1024,6144]{1,0:T(8,128)(2,1)} fusion(bf16[2048,1024]{0,1:T(8,128)(2,1)} %get-tuple-element.17, f32[2048]{0:T(1024)S(1)} %copy-done.13, bf16[2048,6144]{1,0:T(8,128)(2,1)} %convolution_convert_fusion.1, f32[2048,6144]{1,0:T(8,128)} %fusion.11), kind=kOutput, calls=%fused_computation.49 | convolution fusion | flops 25870467072 | bytes 92282880 | tf_op jit(solution)/shard_map/dot_general | solution.py:11
  771.3 0.0 reduce-scatter.13.cloned.1.call-update
  771.3 0.0 reduce-scatter.9.cloned.1.call-start
  771.3 32.4 %convolution_convert_fusion.5 = bf16[1024,6144]{1,0:T(8,128)(2,1)} fusion(bf16[2048,6144]{1,0:T(8,128)(2,1)} %get-tuple-element.18, bf16[2048,1024]{0,1:T(8,128)(2,1)} %get-tuple-element.17, f32[2048]{0:T(1024)S(1)} %copy-done.13), kind=kOutput, calls=%fused_computation.51 | convolution fusion | flops 25782386688 | bytes 41951232 | tf_op jit(solution)/shard_map/dot_general | solution.py:11
  803.7 0.0 reduce-scatter.9.cloned.1.call-update
  803.8 0.0 reduce-scatter.7.cloned.1.call-start
  803.8 0.6 copy-done.9
  804.4 32.7 %convolution_convert_fusion.6 = bf16[1024,6144]{1,0:T(8,128)(2,1)} fusion(bf16[2048,6144]{1,0:T(8,128)(2,1)} %get-tuple-element.22, bf16[1,2048,1024]{1,2,0:T(8,128)(2,1)} %copy.10, f32[2048]{0:T(1024)S(1)} %copy-done.9), kind=kOutput, calls=%fused_computation.52 | convolution fusion | flops 25782386688 | bytes 41951232 | tf_op jit(solution)/shard_map/dot_general | solution.py:11
  837.2 37.9 %fusion.21 = f32[2048,1024]{0,1:T(8,128)} fusion(bf16[1,1024,6144]{2,1,0:T(8,128)(2,1)} %all-gather.15.cloned.1.call-done, bf16[2048,6144]{1,0:T(8,128)(2,1)} %get-tuple-element.23, f32[2048,6144]{1,0:T(8,128)} %fusion.27), kind=kOutput, calls=%fused_computation.39 | convolution fusion | flops 25857884160 | bytes 96468992 | tf_op jit(solution)/shard_map/dot_general | solution.py:11
  875.1 35.7 %fusion.32 = (f32[2048]{0:T(1024)S(1)}, f32[2048,1024]{0,1:T(8,128)}) fusion(bf16[1,2048,1024]{1,2,0:T(8,128)(2,1)S(1)} %copy-done, f32[2048,1024]{0,1:T(8,128)} %fusion.21, bf16[2048,6144]{1,0:T(8,128)(2,1)} %get-tuple-element.22, bf16[1,1024,6144]{2,1,0:T(8,128)(2,1)} %all-gather.13.cloned.1.call-done), kind=kOutput, calls=%fused_computation.55 | convolution fusion | flops 25778190336 | bytes 58728448 | tf_op jit(solution)/shard_map/dot_general | solution.py:11
  910.9 6.2 fusion.42
  917.1 6.4 copy.11
  923.5 2.7 pad_maximum_fusion.2
  926.1 33.7 %reduce-scatter.13.cloned.1.call-done = bf16[64,6144]{1,0:T(8,128)(2,1)} async-done(((bf16[1024,6144]{1,0:T(8,128)(2,1)}), bf16[64,6144]{1,0:T(8,128)(2,1)}) %reduce-scatter.13.cloned.1.call-update) | async-done | bytes 786448 | tf_op jit(solution)/shard_map/reduce_scatter | solution.py:32
  959.8 2.7 pad_maximum_fusion.1
  962.5 92.4 %reduce-scatter.9.cloned.1.call-done = bf16[64,6144]{1,0:T(8,128)(2,1)} async-done(((bf16[1024,6144]{1,0:T(8,128)(2,1)}), bf16[64,6144]{1,0:T(8,128)(2,1)}) %reduce-scatter.9.cloned.1.call-update) | async-done | bytes 786448 | tf_op jit(solution)/shard_map/reduce_scatter | solution.py:32
  1054.9 95.0 %reduce-scatter.7.cloned.1.call-done = bf16[64,6144]{1,0:T(8,128)(2,1)} async-done(((bf16[1024,6144]{1,0:T(8,128)(2,1)}), bf16[64,6144]{1,0:T(8,128)(2,1)}) %reduce-scatter.7.cloned.1.call-update) | async-done | bytes 786448 | tf_op jit(solution)/shard_map/reduce_scatter | solution.py:32
  1149.9 2.7 pad_maximum_fusion
  (37 shorter events, 0.1 us)
Async XLA Ops:
  7.2 68.2 %all-gather.13.cloned.1.call-start = ((), (), s32[]{:S(2)}) async-start(), calls=%async_computation.12 | async-start | bytes 13369344 | tf_op jit(solution)/shard_map/all_gather | solution.py:31
  9.9 130.6 %all-gather.15.cloned.1.call-start = ((), (), s32[]{:S(2)}) async-start(), calls=%async_computation.13 | async-start | bytes 13369344 | tf_op jit(solution)/shard_map/all_gather | solution.py:31
  12.6 192.4 %all-gather.17.cloned.1.call-start = ((), (), s32[]{:S(2)}) async-start(), calls=%async_computation.14 | async-start | bytes 13369344 | tf_op jit(solution)/shard_map/all_gather | solution.py:31
  15.4 254.0 %all-gather.19.cloned.1.call-start = ((), (), s32[]{:S(2)}) async-start(), calls=%async_computation.15 | async-start | bytes 13369344 | tf_op jit(solution)/shard_map/all_gather | solution.py:31
  16.0 318.4 %all-gather.23.cloned.1.call-start = ((), (), s32[]{:S(2)}) async-start(), calls=%async_computation.17 | async-start | bytes 13369344 | tf_op jit(solution)/shard_map/all_gather | solution.py:31
  16.6 382.8 %all-gather.21.cloned.1.call-start = ((), (), s32[]{:S(2)}) async-start(), calls=%async_computation.16 | async-start | bytes 13369344 | tf_op jit(solution)/shard_map/all_gather | solution.py:31
  17.1 906.3 %reduce-scatter.15.cloned.1.call-start = ((), (), s32[]{:S(2)}) async-start(), calls=%async_computation.10 | async-start | bytes 13369344 | tf_op jit(solution)/shard_map/reduce_scatter | solution.py:32
  26.7 0.6 copy-start.5
  27.3 113.2 %copy-start.7 = (f32[2048]{0:T(1024)}, f32[2048]{0:T(1024)S(1)}, u32[]{:S(2)}) copy-start(f32[2048]{0:T(1024)S(1)} %add_rsqrt_fusion.1) | copy-start | bytes 24580
  251.6 52.0 %copy-start.14 = (f32[2048]{0:T(1024)}, f32[2048]{0:T(1024)S(1)}, u32[]{:S(2)}) copy-start(f32[2048]{0:T(1024)S(1)} %get-tuple-element.16) | copy-start | bytes 24580
  251.6 147.8 %copy-start.11 = (f32[2048]{0:T(1024)}, f32[2048]{0:T(1024)S(1)}, u32[]{:S(2)}) copy-start(f32[2048]{0:T(1024)S(1)} %add_rsqrt_fusion) | copy-start | bytes 24580
  467.4 34.9 %copy-start.4 = (bf16[2048,1024]{0,1:T(8,128)(2,1)S(1)}, bf16[2048,1024]{0,1:T(8,128)(2,1)}, u32[]{:S(2)}) copy-start(bf16[2048,1024]{0,1:T(8,128)(2,1)} %get-tuple-element.17) | copy-start | bytes 12582916
  502.2 42.7 %copy-start.15 = (f32[2048]{0:T(1024)S(1)}, f32[2048]{0:T(1024)}, u32[]{:S(2)}) copy-start(f32[2048]{0:T(1024)} %copy-done.14) | copy-start | bytes 24580
  502.2 42.7 %copy-start.1 = (bf16[1,2048,1024]{1,2,0:T(8,128)(2,1)S(1)}, bf16[1,2048,1024]{1,2,0:T(8,128)(2,1)}, u32[]{:S(2)}) copy-start(bf16[1,2048,1024]{1,2,0:T(8,128)(2,1)} %copy.9) | copy-start | bytes 12582916
  502.2 42.7 %copy-start.12 = (f32[2048]{0:T(1024)S(1)}, f32[2048]{0:T(1024)}, u32[]{:S(2)}) copy-start(f32[2048]{0:T(1024)} %copy-done.11) | copy-start | bytes 24580
  549.9 1.9 copy-start.2
  584.2 339.3 %reduce-scatter.17.cloned.1.call-start = ((), (), s32[]{:S(2)}) async-start(), calls=%async_computation.11 | async-start | bytes 13369344 | tf_op jit(solution)/shard_map/reduce_scatter | solution.py:32
  627.0 299.2 %reduce-scatter.11.cloned.1.call-start = ((), (), s32[]{:S(2)}) async-start(), calls=%async_computation.8 | async-start | bytes 13369344 | tf_op jit(solution)/shard_map/reduce_scatter | solution.py:32
  627.0 66.8 %copy-start.8 = (f32[2048]{0:T(1024)S(1)}, f32[2048]{0:T(1024)}, u32[]{:S(2)}) copy-start(f32[2048]{0:T(1024)} %copy-done.7) | copy-start | bytes 24580
  732.1 0.7 copy-start.13
  732.1 227.7 %reduce-scatter.13.cloned.1.call-start = ((), (), s32[]{:S(2)}) async-start(), calls=%async_computation.9 | async-start | bytes 13369344 | tf_op jit(solution)/shard_map/reduce_scatter | solution.py:32
  771.3 283.6 %reduce-scatter.9.cloned.1.call-start = ((), (), s32[]{:S(2)}) async-start(), calls=%async_computation.7 | async-start | bytes 13369344 | tf_op jit(solution)/shard_map/reduce_scatter | solution.py:32
  803.7 0.7 copy-start.9
  803.8 346.1 %reduce-scatter.7.cloned.1.call-start = ((), (), s32[]{:S(2)}) async-start(), calls=%async_computation.6 | async-start | bytes 13369344 | tf_op jit(solution)/shard_map/reduce_scatter | solution.py:32
  837.2 37.9 %copy-start = (bf16[1,2048,1024]{1,2,0:T(8,128)(2,1)S(1)}, bf16[1,2048,1024]{1,2,0:T(8,128)(2,1)}, u32[]{:S(2)}) copy-start(bf16[1,2048,1024]{1,2,0:T(8,128)(2,1)} %copy.10) | copy-start | bytes 12582916
  875.1 35.7 %copy-start.6 = (f32[2048]{0:T(1024)S(1)}, f32[2048]{0:T(1024)}, u32[]{:S(2)}) copy-start(f32[2048]{0:T(1024)} %copy-done.5) | copy-start | bytes 24580
  875.1 35.8 %copy-start.3 = (bf16[2048,1024]{0,1:T(8,128)(2,1)S(1)}, bf16[2048,1024]{0,1:T(8,128)(2,1)}, u32[]{:S(2)}) copy-start(bf16[2048,1024]{0,1:T(8,128)(2,1)} %copy-done.2) | copy-start | bytes 12582916
  875.1 35.8 %copy-start.10 = (f32[2048]{0:T(1024)S(1)}, f32[2048]{0:T(1024)}, u32[]{:S(2)}) copy-start(f32[2048]{0:T(1024)} %copy-done.7) | copy-start | bytes 24580
Sparse Core Ops, SparseCore 0:
  10.2 65.1 all-gather.12
  78.2 62.2 all-gather.14
  142.7 62.2 all-gather.16
  207.1 62.2 all-gather.18
  272.1 62.2 all-gather.22
  337.1 62.2 all-gather.20
  584.3 90.3 reduce-scatter.14
  679.4 90.3 reduce-scatter.16
  774.4 90.4 reduce-scatter.10
  869.4 90.4 reduce-scatter.12
  964.5 90.4 reduce-scatter.8
  1059.4 90.4 reduce-scatter.6

commit v2 on v0

v2 whole, which is shorter than its diff:
```python
import functools

import jax
import jax.numpy as jnp
from jax import lax
from jax.experimental import pallas as pl
from jax.experimental.pallas import tpu as pltpu
from jax.sharding import PartitionSpec as P

BF, F32 = jnp.bfloat16, jnp.float32
MESH = pl.DeviceIdType.MESH
R = 128
D = CW = 8 * R
TT = 256
HT, NT = 8, 16
TB, BT = 2 * TT, NT // 2
T = HT * TT
U = 3
VMEM_LIMIT = 67_043_328

M = 3
ITEMS = [f"{m}0{j}" for j in range(U) for m in "gu"] + [f"d0{j}" for j in range(U)] + [f"{m}1{j}" for j in range(U) for m in "gud"]
NI = len(ITEMS)
PLANES = range(3)
LAST = (HT - 2, HT - 1)
NN, NTR, TN = ((1,), (0,)), ((1,), (1,)), ((0,), (0,))


def triple(n):
    return range(3 * n, 3 * n + 3)


def odd(t):
    return lax.rem(t, 2)


def dot(a, b, dims):
    return lax.dot_general(a, b, (dims, ((), ())), preferred_element_type=F32)


def scale_of(wide):
    return lax.rsqrt(jnp.mean(wide**2, -1, keepdims=True) + 1e-6)


def cols(k, parts=4):
    return slice(k * CW // parts, (k + 1) * CW // parts)


class Place:
    def __init__(self):
        me = lax.axis_index("dp")
        self.c = odd(me)
        p = me // 2
        self.b = [lax.rem(p // 4, 2), lax.rem(p // 2, 2), odd(p)]
        self.partner = (0, me + 1 - 2 * self.c)

    def chip(self, flips):
        b = [1 - v if f else v for v, f in zip(self.b, flips, strict=True)]
        return b[0] * 4 + b[1] * 2 + b[2]

    def neighbour(self, dim):
        return (0, self.chip([dim == d for d in PLANES]) * 2 + self.c)

    def rows(self, q, k):
        flips = [0, 0, 0]
        for j in PLANES:
            flips[(k + j) % 3] = (q >> (2 - j)) & 1
        return pl.ds(pl.multiple_of(self.chip(flips) * R, R), R)

    def greet(self):
        bar = pltpu.get_barrier_semaphore()
        for device in (*map(self.neighbour, PLANES), self.partner):
            pl.semaphore_signal(bar, inc=1, device_id=device, device_id_type=MESH)
        pl.semaphore_wait(bar, 4)


def copy(src, dst, sem):
    return pltpu.make_async_copy(src, dst, sem)


def remote(src, dst, send, recv, device):
    return pltpu.make_async_remote_copy(src, dst, send, recv, device_id=device, device_id_type=MESH)


def arrived(ref, sem):
    copy(ref, ref, sem).wait()


def tile(t, size=None):
    size = size or TT
    return pl.ds(pl.multiple_of(t * size, size), size)


def lanes(p, parity, u):
    return pl.ds(pl.multiple_of(((2 * p + parity) * U + u) * R, R), R)


def each(n, f):
    def body(p, carry):
        f(p)
        return carry

    lax.fori_loop(0, n, body, 0)


class Gather:
    def __init__(self, at, st, w, ssem, rsem):
        self.at, self.st, self.w, self.ssem, self.rsem = at, st, w, ssem, rsem

    def send(self, i, q, j):
        k = i % 3
        rows = self.at.rows(q, k)
        src = self.st.at[i] if q == 0 else self.w.at[i, rows]
        remote(src, self.w.at[i, rows], self.ssem.at[i], self.rsem.at[i, (q | (4 >> j)) - 1], self.at.neighbour((k + j) % 3)).start()

    def wait(self, i, q):
        arrived(self.w.at[i, self.at.rows(q, i % 3)], self.rsem.at[i, q - 1])

    def s0(self, n):
        for j in PLANES:
            for i in triple(n):
                self.send(i, 0, j)

    def s1(self, n):
        with jax.named_scope(f"s1#n={n}"):
            for i in triple(n):
                self.wait(i, 4)
            for j in (1, 2):
                for i in triple(n):
                    self.send(i, 4, j)

    def s2(self, n):
        with jax.named_scope(f"s2#n={n}"):
            for q in (2, 6):
                for i in triple(n):
                    self.wait(i, q)
                    self.send(i, q, 2)

    def s3(self, n):
        with jax.named_scope(f"s3#n={n}"):
            for q in (1, 5, 3, 7):
                for i in triple(n):
                    self.wait(i, q)

    def drain(self, first, last):
        for i in range(first, last):
            arrived(self.w.at[i, pl.ds(0, 7 * R)], self.ssem.at[i])


class Reduce:
    def __init__(self, at, acc, near, sbuf, ibuf, obuf, outs, ssem, rsem, osem, psem, qsem, credit):
        self.at, self.acc, self.near, self.sbuf, self.ibuf, self.obuf, self.outs = at, acc, near, sbuf, ibuf, obuf, outs
        self.ssem, self.rsem, self.osem, self.psem, self.qsem, self.credit = ssem, rsem, osem, psem, qsem, credit

    def _send(self, m, s, u):
        @pl.when(u > 0)
        def _():
            pl.semaphore_wait(self.credit.at[m, s], 1)

        remote(self.sbuf[s].at[m], self.ibuf[s].at[m], self.ssem.at[m, s], self.rsem.at[m, s], self.at.neighbour((m + s) % 3)).start()

    def _sent(self, m, s, u):
        @pl.when(u > 0)
        def _():
            arrived(self.sbuf[s].at[m], self.ssem.at[m, s])

    def _taken(self, m, s, u):
        @pl.when(u < U - 1)
        def _():
            pl.semaphore_signal(self.credit.at[m, s], inc=1, device_id=self.at.neighbour((m + s) % 3), device_id_type=MESH)

    def step0(self, u):
        for m in range(M):
            self._sent(m, 0, u)
            for q in range(4, 8):
                self.sbuf[0][m, pl.ds((q - 4) * R, R), :] = self.acc[m, self.at.rows(q, m), :].astype(BF)
            self._send(m, 0, u)
        for m in range(M):
            for q in range(4):
                self.near[0][m, pl.ds(q * R, R), :] = self.acc[m, self.at.rows(q, m), :]

    def step1(self, u):
        for m in range(M):
            self._sent(m, 1, u)
            arrived(self.ibuf[0].at[m], self.rsem.at[m, 0])
            far, keep = pl.ds(2 * R, 2 * R), pl.ds(0, 2 * R)
            self.sbuf[1][m] = (self.near[0][m, far, :] + self.ibuf[0][m, far, :].astype(F32)).astype(BF)
            self._send(m, 1, u)
            self.near[1][m] = self.near[0][m, keep, :] + self.ibuf[0][m, keep, :].astype(F32)
            self._taken(m, 0, u)

    def step2(self, u):
        for m in range(M):
            self._sent(m, 2, u)
            arrived(self.ibuf[1].at[m], self.rsem.at[m, 1])
            far, keep = pl.ds(R, R), pl.ds(0, R)
            self.sbuf[2][m] = (self.near[1][m, far, :] + self.ibuf[1][m, far, :].astype(F32)).astype(BF)
            self._send(m, 2, u)
            self.near[1][m, keep, :] = self.near[1][m, keep, :] + self.ibuf[1][m, keep, :].astype(F32)
            self._taken(m, 1, u)

    def _halves(self, m):
        half = R // 2
        return [self.obuf.at[m, pl.ds(pl.multiple_of(v * half, half), half)] for v in (self.at.c, 1 - self.at.c)]

    def _out(self, m, u):
        if m == 2:
            copy(self.obuf.at[2], self.outs[2].at[u], self.osem.at[2]).start()
            return
        mine, other = self._halves(m)

        def put(p):
            block, there = pl.ds(pl.multiple_of(p * R, R), R), self.outs[m].at[:, lanes(p, self.at.c, u)]
            copy(mine.at[:, block], there, self.osem.at[m]).start()
            remote(other.at[:, block], there, self.psem.at[m], self.qsem.at[m, u], self.at.partner).start()

        each(8, put)

    def _out_done(self, m):
        if m == 2:
            arrived(self.obuf.at[2], self.osem.at[2])
            return
        mine, other = self._halves(m)
        arrived(mine, self.osem.at[m])
        arrived(other, self.psem.at[m])

    def step3(self, u):
        for m in range(M):
            @pl.when(u > 0)
            def _(m=m):
                self._out_done(m)

            arrived(self.ibuf[2].at[m], self.rsem.at[m, 2])
            self.obuf[m] = (self.near[1][m, pl.ds(0, R), :] + self.ibuf[2][m].astype(F32)).astype(BF)
            self._taken(m, 2, u)
            self._out(m, u)

    def freed(self):
        for m in range(M):
            arrived(self.sbuf[0].at[m], self.ssem.at[m, 0])

    def drain(self):
        for m in range(M):
            self._out_done(m)
            for s in (1, 2):
                arrived(self.sbuf[s].at[m], self.ssem.at[m, s])
        for m in range(2):
            for u in range(U):
                arrived(self._halves(m)[0], self.qsem.at[m, u])


def gradients(gate, up, dhid):
    dhid = dhid.astype(BF).astype(F32)
    sig = jax.nn.sigmoid(gate)
    silu = gate * sig
    return (dhid * up * (sig + silu * (1 - sig))).astype(BF), (dhid * silu).astype(BF), silu


def back_chunks(red, acc, wbuf, slot_of, ta, td, kept, tg, load, isem, hbm_out, osem, parts, hid, ticks):
    last = U * BT
    ins = (ta, td, *(kept or ()))

    def place(it):
        return it // BT, lax.rem(it, BT)

    def stores(it, s):
        u, t = place(it)
        return [copy(tg[n].at[s], hbm_out.at[n, u, tile(t, TB)], osem.at[n, s]) for n in range(2)]

    load(0, 0, 0)

    def body(it, carry):
        (u, t), s = place(it), odd(it)
        with jax.named_scope("b_wait"):
            for n, ref in enumerate(ins):
                arrived(ref.at[s], isem.at[n, s])
            for when, group in ticks.items():
                @pl.when(t == when)
                def _(group=group):
                    for tick in group:
                        tick(u)

            @pl.when(it > 1)
            def _():
                for store in stores(it - 2, s):
                    store.wait()

            load(*place(lax.rem(it + 1, last)), 1 - s)
        base = slot_of(u)

        def front(k):
            c = cols(k)
            dhid = dot(td[s], wbuf[base if kept else base + 2, c, :], NTR)
            if kept:
                gate, up = kept[0][s, :, c], kept[1][s, :, c]
            else:
                gate, up = dot(ta[s], wbuf[base, :, c], NN), dot(ta[s], wbuf[base + 1, :, c], NN)
            tg[0][s, :, c], tg[1][s, :, c], silu = gradients(gate, up, dhid)
            hid[:, c] = (silu * up).astype(BF)

        def add(m, r, c, term):
            acc[m, r, c] = jnp.where(t == 0, 0.0, acc[m, r, c]) + term

        def back(k):
            c, every = cols(k, parts), slice(None)
            for n in range(2):
                add(n, every, c, dot(ta[s], tg[n][s, :, c], TN))
            add(2, c, every, dot(hid[:, c], td[s], TN))

        with jax.named_scope("b_mm"):
            per = 4 // parts
            for k in range(4):
                front(k)
                if k >= per and k % per == 0:
                    back(k // per - 1)
            back(parts - 1)
        for store in stores(it, s):
            store.start()

        @pl.when(t == BT - 1)
        def _():
            with jax.named_scope("step0"):
                red.step0(u)

        return carry

    lax.fori_loop(0, last, body, 0)
    for n, ref in enumerate(ins):
        arrived(ref.at[last % 2], isem.at[n, last % 2])
    for it in (last - 2, last - 1):
        for store in stores(it, it % 2):
            store.wait()


def da_tiles(ta, td, tg, sb):
    def of(b, s):
        if b < 4:
            return (ta, td)[b // 2].at[s, tile(b % 2)]
        return tg[b - 4].at[0, tile(s)] if b < 6 else sb.at[b - 6, tile(s)]

    return of


def landing(acc, t):
    per = D // TT
    return acc.at[t // per, tile(lax.rem(t, per))]


def back_to_h(at, acc, wbuf, gslots, uslots, tiles, hbm_in, ksem, fbuf, fsem, lsem, h_in, dh_in, esem, results, red, ticks):
    def loads(i, s):
        row = lax.rem(i + HT, NT)
        return [copy(hbm_in.at[b % 2, b // 2, tile(row)], tiles(b, s), ksem.at[s, b]) for b in range(2 * U)]

    def eloads(t, s):
        return [copy(src.at[tile(t)], tiles(2 * U + n, s), esem.at[n, s]) for n, src in enumerate((h_in, dh_in))]

    def fsend(t, s):
        return remote(fbuf(s), landing(acc, t), fsem.at[s], lsem.at[t], at.partner)

    def results_done(t, s):
        local, *far = results(t, s)
        local.wait()
        for out in far:
            out.wait_send()

    for ld in loads(0, 0):
        ld.start()

    def body(i, carry):
        s, t = odd(i), i - HT
        for when, tick in ticks:
            pl.when(i == when)(tick)

        @pl.when((i > 1) & (i < HT + 2))
        def _():
            fsend(i - 2, s).wait_send()

        @pl.when(i == HT)
        def _():
            red.freed()
            for ld in eloads(0, 0):
                ld.start()

        for ld in loads(i, s):
            ld.wait()
        for ld in loads(lax.rem(i + 1, NT), 1 - s):
            ld.start()
        into = fbuf(s)
        for k in range(4):
            c = cols(k)
            terms = [dot(tiles(b, s)[...], wbuf[(gslots, uslots)[b % 2][b // 2], c, :], NTR) for b in range(2 * U)]
            into[:, c] = functools.reduce(jnp.add, terms)

        @pl.when(i < HT)
        def _():
            fsend(i, s).start()

        @pl.when(i >= HT)
        def _():
            for ld in eloads(t, s):
                ld.wait()
            land = landing(acc, t)
            arrived(land, lsem.at[t])
            da = into[...] + land[...]
            wide = tiles(2 * U, s)[...].astype(F32)
            scale = scale_of(wide)
            inner = jnp.mean(wide * da, -1, keepdims=True)
            dh = tiles(2 * U + 1, s)[...].astype(F32) + (scale * da - wide * (scale**3 * inner))
            tiles(2 * U, s)[...] = dh.astype(BF)
            for out in results(t, s):
                out.start()

            @pl.when(t > 0)
            def _():
                results_done(t - 1, 1 - s)

            @pl.when(t + 1 < HT)
            def _():
                for ld in eloads(t + 1, 1 - s):
                    ld.start()

        return carry

    with jax.named_scope("back_to_h"):
        lax.fori_loop(0, NT, body, 0)
    for ld in loads(0, 0):
        ld.wait()
    results_done(HT - 1, (HT - 1) % 2)


def fetcher(w, wbuf, wsem):
    def fetch(keys, slots):
        for key, slot in zip(keys.split(), map(int, slots), strict=True):
            copy(w.at[ITEMS.index(key)], wbuf.at[slot], wsem.at[slot]).start()

    def fetched(slots):
        for slot in map(int, slots):
            arrived(wbuf.at[slot], wsem.at[slot])

    return fetch, fetched


def rs_ticks(red):
    return {1: lambda u: pl.when(u > 1)(lambda: red.step2(u - 2)), 6: lambda u: rs_middle(red, u)}


def rs_middle(red, u):
    pl.when(u > 1)(lambda: red.step3(u - 2))
    pl.when(u > 0)(lambda: red.step1(u - 1))


def joined(ticks, red):
    all_of = {t: [f] for t, f in rs_ticks(red).items()}
    for (u, t), f in ticks.items():
        all_of.setdefault(t, []).append(lambda now, u=u, f=f: pl.when(now == u)(f))
    return all_of


def rs_last(red):
    return [(2, lambda: red.step2(U - 2)), (9, lambda: red.step3(U - 2)), (9, lambda: red.step1(U - 1)), (13, lambda: red.step2(U - 1))]


def first_kernel(
    x, dy, wg, wu, wd,
    w, a0, gate, up, hid, h1, a1, dyall, dgu, dh1, og, ou, od,
    st, wbuf, acc, near0, near1, sb0, sb1, sb2, ib0, ib1, ib2, obuf, ta, td, tg0, tg1, hb,
    rs_s, rs_r, rs_o, rs_p, rs_q, credit, isem, osem, ksem, fsem, lsem, esem, free, wsem,
    g_s, g_r, st_l, st_r, own, xs, xr,
):
    at = Place()
    at.greet()
    gather = Gather(at, st, w, g_s, g_r)
    c, half = at.c, R // 2
    halves = [pl.ds(pl.multiple_of(v * half, half), half) for v in (c, 1 - c)]

    def stage(n):
        for i in triple(n):
            m, l, j = ITEMS[i][0], int(ITEMS[i][1]), int(ITEMS[i][2])
            if m == "d":
                copy(wd.at[l, pl.ds(j * R, R)], st.at[i], st_l.at[i]).start()
                continue

            def put(p, i=i, src=(wg if m == "g" else wu).at[l], j=j):
                there = st.at[i, halves[0], pl.ds(pl.multiple_of(p * R, R), R)]
                remote(src.at[:, lanes(p, 1 - c, j)], there, st_l.at[NI + i], st_r.at[i], at.partner).start()
                copy(src.at[:, lanes(p, c, j)], there, st_l.at[i]).start()

            each(8, put)

    def begin(n):
        for i in triple(n):
            if ITEMS[i][0] == "d":
                arrived(st.at[i], st_l.at[i])
            else:
                arrived(st.at[i, halves[0]], st_l.at[i])
                arrived(st.at[i, halves[1]], st_r.at[i])
            copy(st.at[i], w.at[i, at.rows(0, i % 3)], own.at[i]).start()
        gather.s0(n)

    def whole(n):
        gather.s3(n)
        for i in triple(n):
            arrived(st.at[i], own.at[i])

    fetch, fetched = fetcher(w, wbuf, wsem)

    stage(0)
    begin(0)
    for n in range(1, NI // 3):
        stage(n)
    dy_out = remote(dy, dyall.at[pl.ds(T, T)], xs.at[0], xr.at[0], at.partner)
    dy_out.start()

    def xload(t, s):
        return copy(x.at[tile(t)], tg0.at[0, tile(s)], isem.at[3, s])

    def both(t, s, buf, dst, n):
        return copy(buf, dst.at[tile(t)], osem.at[0, s]), remote(buf, dst.at[tile(t + HT)], osem.at[1, s], xr.at[n], at.partner)

    def both_done(*args):
        local, far = both(*args)
        local.wait()
        far.wait_send()

    def norm_of(s):
        return td.at[0, tile(s)]

    def dyload(t, s):
        return copy(dy.at[tile(t)], td.at[1, tile(s)], isem.at[1, s])

    def dystore(t, s):
        return copy(td.at[1, tile(s)], dyall.at[tile(t)], ksem.at[s, 1])

    xload(0, 0).start()

    def norm_tile(t, carry):
        s = odd(t)
        xload(t, s).wait()

        @pl.when(t + 1 < HT)
        def _():
            xload(t + 1, 1 - s).start()

        @pl.when(t >= 2)
        def _():
            both_done(t - 2, s, norm_of(s), a0, 1)
            dystore(t - 2, s).wait()

        pl.when(t == 4)(lambda: gather.s1(0))
        dyload(t, s).start()
        wide = tg0[0, tile(s), :].astype(F32)
        norm_of(s)[...] = (wide * scale_of(wide)).astype(BF)
        dyload(t, s).wait()
        for out in (*both(t, s, norm_of(s), a0, 1), dystore(t, s)):
            out.start()
        return carry

    with jax.named_scope("norm"):
        lax.fori_loop(0, HT, norm_tile, 0)
    for t in LAST:
        both_done(t, t % 2, norm_of(t % 2), a0, 1)
        dystore(t, t % 2).wait()
    arrived(a0.at[pl.ds(T, T)], xr.at[1])
    gather.s2(0)
    begin(1)

    def aload(t, s):
        return copy(a0.at[tile(lax.rem(t, BT), TB)], ta.at[s], isem.at[0, s])

    def stores(it, s):
        j, rows = it // BT, tile(lax.rem(it, BT), TB)
        return [
            copy(acc.at[2, tile(s, TB)], gate.at[j, rows], osem.at[0, s]),
            copy(near0.at[s], up.at[j, rows], osem.at[1, s]),
            copy(td.at[s], hid.at[j, rows], ksem.at[s, 0]),
        ]

    def second():
        gather.s2(1)
        begin(2)
        whole(1)
        fetch("g01 u01 g02 u02", "2345")
        fetched("23")

    def third():
        gather.s2(2)
        begin(3)

    ticks = {3: lambda: gather.s1(1), BT: second, 12: lambda: gather.s1(2), 2 * BT: lambda: fetched("45"), 18: third}

    def gate_up(it, carry):
        j, s = it // BT, odd(it)
        aload(it, s).wait()
        for when, tick in ticks.items():
            pl.when(it == when)(tick)

        @pl.when(it > 1)
        def _():
            for store in stores(it - 2, s):
                store.wait()

        aload(it + 1, 1 - s).start()
        for k in range(4):
            cc = cols(k)
            g, v = (dot(ta[s], wbuf[2 * j + n, :, cc], NN) for n in range(2))
            acc[2, tile(s, TB), cc] = g
            near0[s, :, cc] = v
            td[s, :, cc] = (jax.nn.silu(g) * v).astype(BF)
        for store in stores(it, s):
            store.start()
        return carry

    aload(0, 0).start()
    whole(0)
    fetch("g00 u00", "01")
    fetched("01")
    with jax.named_scope("gate_up"):
        lax.fori_loop(0, U * BT, gate_up, 0)
    aload(0, 0).wait()
    for it in range(2):
        for store in stores(U * BT - 2 + it, it):
            store.wait()

    def hloads(i, s):
        row = lax.rem(i + HT, NT)
        return [copy(hid.at[j, tile(row)], sb0.at[j, tile(s)], isem.at[j, s]) for j in range(U)]

    def sums(s):
        return acc.at[2, tile(s)]

    def fsend(t, s):
        return remote(sums(s), landing(acc, t), fsem.at[s], lsem.at[t], at.partner)

    for ld in hloads(0, 0):
        ld.start()
    whole(2)
    fetch("d00 d01 d02", "012")
    fetched("012")
    gather.s1(3)
    xload(0, 0).start()

    def down(i, s):
        for ld in hloads(i, s):
            ld.wait()

        @pl.when(i + 1 < NT)
        def _():
            for ld in hloads(i + 1, 1 - s):
                ld.start()

        for k in range(4):
            cc = cols(k)
            terms = [dot(sb0[j, tile(s), :], wbuf[j, :, cc], NN) for j in range(U)]
            sums(s)[:, cc] = functools.reduce(jnp.add, terms)

    def hout(t, s):
        return copy(td.at[1, tile(s)], h1.at[tile(t)], ksem.at[s, 0])

    def down_tile(i, carry):
        s = odd(i)

        @pl.when((i > 1) & (i < HT + 2))
        def _():
            fsend(i - 2, s).wait_send()

        @pl.when(i == HT + 1)
        def _():
            gather.s2(3)
            begin(4)

        down(i, s)

        @pl.when(i < HT)
        def _():
            fsend(i, s).start()

        @pl.when(i >= HT)
        def _():
            t = i - HT
            xload(t, s).wait()

            @pl.when(t + 1 < HT)
            def _():
                xload(t + 1, 1 - s).start()

            @pl.when(t > 1)
            def _():
                both_done(t - 2, s, norm_of(s), a1, 2)
                hout(t - 2, s).wait()

            land = landing(acc, t)
            arrived(land, lsem.at[t])
            h = tg0[0, tile(s), :] + (sums(s)[...] + land[...]).astype(BF)
            td[1, tile(s), :] = h
            wide = h.astype(F32)
            norm_of(s)[...] = (wide * scale_of(wide)).astype(BF)
            for out in (*both(t, s, norm_of(s), a1, 2), hout(t, s)):
                out.start()

        return carry

    with jax.named_scope("down"):
        lax.fori_loop(0, NT, down_tile, 0)
    for t in LAST:
        both_done(t, t % 2, norm_of(t % 2), a1, 2)
        hout(t, t % 2).wait()
    whole(3)
    fetch("g10 u10 d10", "345")
    arrived(dyall.at[pl.ds(T, T)], xr.at[0])
    dy_out.wait_send()
    arrived(a1.at[pl.ds(T, T)], xr.at[2])
    fetched("345")

    red = Reduce(at, acc, (near0, near1), (sb0, sb1, sb2), (ib0, ib1, ib2), obuf, (og, ou, od), rs_s, rs_r, rs_o, rs_p, rs_q, credit)

    def fifth():
        gather.s2(4)
        begin(5)

    def weights1():
        whole(4)
        fetch("g11 u11 d11", "012")

    def weights2():
        whole(5)
        fetch("g12 u12 d12", "345")

    ticks = {
        (0, 1): lambda: gather.s1(4),
        (0, 3): fifth,
        (0, 6): weights1,
        (0, 7): lambda: gather.s1(5),
        (1, 0): lambda: fetched("012"),
        (1, 2): lambda: gather.s2(5),
        (1, 6): weights2,
        (2, 0): lambda: fetched("345"),
        (2, 1): lambda: fetch("g10 u10 g11", "012"),
    }

    def load(u, t, s):
        for n, (src, dst) in enumerate(((a1, ta), (dyall, td))):
            copy(src.at[tile(t, TB)], dst.at[s], isem.at[n, s]).start()

    back_chunks(red, acc, wbuf, lambda u: 3 * odd(u + 1), ta, td, None, (tg0, tg1), load, isem, dgu, osem, 4, hb, joined(ticks, red))
    pl.semaphore_signal(free, inc=1, device_id=at.partner, device_id_type=MESH)
    fetch("u11", "5")
    fetched("0125")
    pl.semaphore_wait(free, 1)

    tiles = da_tiles(ta, td, (tg0, tg1), sb0)

    def results(t, s):
        return both(t, s, tiles(2 * U, s), dh1, 3)

    back_to_h(at, acc, wbuf, (0, 2, 3), (1, 5, 4), tiles, dgu, ksem, sums, fsem, lsem, h1, dy, esem, results, red, rs_last(red))
    with jax.named_scope("tail"):
        red.step3(U - 1)
        arrived(dh1.at[pl.ds(T, T)], xr.at[3])
        gather.drain(0, NI)
        for i, item in enumerate(ITEMS):
            if item[0] != "d":
                arrived(st.at[i, halves[0]], st_l.at[NI + i])
        red.drain()


def second_kernel(
    x, w, a0, gate, up, dh,
    dx, dgu, og, ou, od,
    wbuf, acc, near0, near1, sb0, sb1, sb2, ib0, ib1, ib2, obuf, ta, td, tg0, tg1, hb,
    rs_s, rs_r, rs_o, rs_p, rs_q, credit, isem, osem, ksem, fsem, lsem, esem, free, wsem,
    gt0, gt1,
):
    at = Place()

    fetch, fetched = fetcher(w, wbuf, wsem)

    fetch("d00", "0")
    at.greet()
    red = Reduce(at, acc, (near0, near1), (sb0, sb1, sb2), (ib0, ib1, ib2), obuf, (og, ou, od), rs_s, rs_r, rs_o, rs_p, rs_q, credit)

    def load(u, t, s):
        for n, (src, dst) in enumerate(((a0, ta), (dh, td), (gate.at[u], gt0), (up.at[u], gt1))):
            copy(src.at[tile(t, TB)], dst.at[s], isem.at[n, s]).start()

    ticks = {
        (0, 0): lambda: fetched("0"),
        (0, 1): lambda: fetch("d01 d02", "12"),
        (0, 3): lambda: fetch("g00 u00 g01", "345"),
        (0, 7): lambda: fetched("12"),
        (1, 1): lambda: fetch("u01", "0"),
        (2, 1): lambda: fetch("g02", "1"),
    }
    back_chunks(red, acc, wbuf, lambda u: u, ta, td, (gt0, gt1), (tg0, tg1), load, isem, dgu, osem, 2, hb, joined(ticks, red))
    pl.semaphore_signal(free, inc=1, device_id=at.partner, device_id_type=MESH)
    fetch("u02", "2")
    fetched("345012")
    pl.semaphore_wait(free, 1)

    tiles = da_tiles(ta, td, (tg0, tg1), sb0)

    def results(t, s):
        return [copy(tiles(2 * U, s), dx.at[tile(t)], osem.at[0, s])]

    back_to_h(at, acc, wbuf, (3, 5, 1), (4, 0, 2), tiles, dgu, ksem, lambda s: gt0.at[s, pl.ds(0, TT)], fsem, lsem, x, dh, esem, results, red, rs_last(red))
    with jax.named_scope("tail"):
        red.step3(U - 1)
        red.drain()


def solution(mesh):
    f32, bf = (lambda *s: jax.ShapeDtypeStruct(s, F32)), (lambda *s: jax.ShapeDtypeStruct(s, BF))
    dma, regular = pltpu.SemaphoreType.DMA, pltpu.SemaphoreType.REGULAR
    grads = [bf(R // 2, 2 * U * CW), bf(R // 2, 2 * U * CW), bf(U, R, D)]
    spread = [(3, 4 * R, D), (3, 2 * R, D), (3, R, D)]
    shared = [
        pltpu.VMEM((6, D, CW), BF),
        pltpu.VMEM((3, D, D), F32),
        *(pltpu.VMEM(s, F32) for s in spread[:2]),
        *(pltpu.VMEM(s, BF) for s in spread),
        *(pltpu.VMEM(s, BF) for s in spread),
        pltpu.VMEM((3, R, D), BF),
        *[pltpu.VMEM((2, TB, D), BF)] * 4,
        pltpu.VMEM((TB, CW), BF),
        dma((3, 3)), dma((3, 3)), dma((3,)), dma((2,)), dma((2, U)), regular((3, 3)),
        dma((4, 2)), dma((2, 2)), dma((2, 6)), dma((2,)), dma((HT,)), dma((2, 2)), regular, dma((6,)),
    ]

    def call(kernel, number, outs, scratch, *args):
        anywhere = pl.BlockSpec(memory_space=pl.ANY)
        return pl.pallas_call(
            kernel,
            out_shape=outs,
            in_specs=[anywhere] * len(args),
            out_specs=[anywhere] * len(outs),
            scratch_shapes=scratch,
            compiler_params=pltpu.CompilerParams(collective_id=number, has_side_effects=True, vmem_limit_bytes=VMEM_LIMIT),
        )(*args)

    def body(x, dy, w_gate, w_up, w_down):
        x, dy = x[0], dy[0]

        hidden = [f32(U, 2 * T, CW), f32(U, 2 * T, CW), bf(U, 2 * T, CW)]
        dgu = bf(2, U, 2 * T, CW)
        w, a0, gate, up, _, _, _, _, _, dh, *g1 = call(
            first_kernel, 0,
            [bf(NI, D, CW), bf(2 * T, D), *hidden, bf(T, D), *[bf(2 * T, D)] * 2, dgu, bf(2 * T, D), *grads],
            [
                pltpu.VMEM((NI, R, CW), BF), *shared,
                dma((NI,)), dma((NI, 7)), dma((2 * NI,)), dma((NI,)), dma((NI,)), dma((1,)), dma((4,)),
            ],
            x, dy, w_gate, w_up, w_down,
        )
        dx, _, *g0 = call(
            second_kernel, 1,
            [bf(T, D), dgu, *grads],
            [*shared, *[pltpu.VMEM((2, TB, CW), F32)] * 2],
            x, w, a0, gate, up, dh,
        )
        downs = jnp.stack([g0[2], g1[2]]).reshape(2, U * R, D)
        return dx[None], jnp.stack([g0[0], g1[0]]), jnp.stack([g0[1], g1[1]]), downs

    rows, data = P(None, "dp", None), P(("rep", "dp"), None, None)
    return jax.shard_map(body, mesh=mesh, in_specs=(data, data, rows, rows, rows), out_specs=(data, rows, rows, rows), check_vma=False)
```

time: 3000 us -> 632 us (0.21)
  starting transfers between devices: 1040 us -> 0 us
  matrix products: 904 us -> 0 us
  Pallas kernels: 0 us -> 623 us
  waiting for transfers between devices: 528 us -> 0 us
  other arithmetic: 341 us -> 5.22 us
  local copies, waits for them, and re-layouts: 160 us -> 2.03 us
    dot_general x119 -> x0, starting transfers between devices: 1040 us -> none  [the longest x51 441 us: matmul(): jnp.dot(a, w, preferred_element_type=jnp.float32).astype(jnp.bfloat16)]
    dot_general x66 -> x0, matrix products: 904 us -> none  [the longest x20 344 us: layer(): up = jnp.dot(a, w['w_up'], preferred_element_type=jnp.float32)]
    pallas_call x0 -> x2, Pallas kernels: none -> 623 us  [call(): pl.pallas_call(kernel, out_shape=outs, in_specs=[anywhere] * len(args), o...]
    dot_general x119 -> x0, waiting for transfers between devices: 528 us -> none  [the longest x51 252 us: matmul(): jnp.dot(a, w, preferred_element_type=jnp.float32).astype(jnp.bfloat16)]
    dot_general x96 -> x0, other arithmetic: 246 us -> none
    unnamed x64 -> x7, local copies, waits for them, and re-layouts: 93.1 us -> 2.03 us
    dot_general x18 -> x0, local copies, waits for them, and re-layouts: 61.7 us -> none  [matmul(): jnp.dot(a, w, preferred_element_type=jnp.float32).astype(jnp.bfloat16)]
    mul x3 -> x0, other arithmetic: 58.3 us -> none  [the longest x1 58.3 us: layer(): jax.nn.silu(gate) * up]
  transfers between devices with their start and end apart: 124 -> 0, of which waited for: 60 -> 0; matrix products, arithmetic and copies ran while one was open for 43% -> 0% of each run, Pallas kernels for 0% -> 0%
where the time goes in v2:
time: 632 us; the launch traced here: 631 us
  Pallas kernels  623 us (99%)
    pallas_call x2, Pallas kernels, call(): pl.pallas_call(kernel, out_shape=outs, in_specs=[anywhere] * len(args), o...  623 us

profile of v2, /device:TPU:0, one launch (start us, length us, event | category | flops | bytes accessed | tf_op | source)
XLA Modules:
  0.0 631.2 jit_solution(14010667273167582613)
XLA Ops:
  0.6 420.9 %shard_map.84 = (bf16[18,1024,1024]{2,1,0:T(8,128)(2,1)}, bf16[4096,1024]{1,0:T(8,128)(2,1)}, f32[3,4096,1024]{2,1,0:T(8,128)}, f32[3,4096,1024]{2,1,0:T(8,128)}...) custom-call(bf16[2048,1024]{1,0:T(8,128)(2,1)} %bitcast.9, ...), custom_call_target="tpu_custom_call" | custom-call | tf_op jit(solution)/shard_map/pallas_call | solution.py:830
  421.5 202.4 %shard_map.85 = (bf16[2048,1024]{1,0:T(8,128)(2,1)}, bf16[2,3,4096,1024]{3,2,1,0:T(8,128)(2,1)}, bf16[64,6144]{1,0:T(8,128)(2,1)}, bf16[64,6144]{1,0:T(8,128)(2,1)}, bf16[3,128,1024]{2,1,0:T(8,128)(2,1)}) custom-call(bf16[2048,1024]{1,0:T(8,128)(2,1)} %bitcast.10, bf16[18,1024,1024]{2,1,0:T(8,128)(2,1)} %get-tuple-element.16.w, ...), custom_call_target="tpu_custom_call" | custom-call | tf_op jit(solution)/shard_map/pallas_call | solution.py:830
  624.0 0.0 copy-start.1
  624.0 0.0 copy-start.2
  624.0 0.0 copy-start
  624.0 3.9 pad_maximum_fusion
  627.9 0.0 copy-done.1
  627.9 0.0 copy-done.2
  627.9 1.3 pad_maximum_fusion.2
  629.2 0.0 copy-done
  629.2 2.0 copy.10
Async XLA Ops:
  624.0 4.0 copy-start.1
  624.0 4.0 copy-start.2
  624.0 5.2 copy-start
